TPU v7x, 32 devices: a whole 2x2x4 slice. The times are simulated.
32 devices in a mesh: dp: 2 (over x), fsdp: 4 (over z), tensor: 4 (over y, core).
Axes of the slice: x: 2, y: 2, z: 4, core: 2. Of those that a mesh axis runs over, the one named last changes fastest.
Arguments:
- grads: bfloat16 [2, 4, 16, 53248], P('dp', 'fsdp', None, 'tensor'), may hold values from -64 to 64, as said below
- params: bfloat16 [16, 53248], P('fsdp', 'tensor'), may hold values from -0.119628906 to 0.119628906
- moment_norm: bfloat16 [16, 53248], P('fsdp', 'tensor'), may hold values from -1 to 1
- moment_scale: float32 [16, 416], P('fsdp', 'tensor'), may hold values from 0.05 to 0.5
- second_norm: bfloat16 [16, 53248], P('fsdp', 'tensor'), may hold values from 0.049804688 to 1
- second_rows: float32 [16], P('fsdp'), may hold values from 0.01 to 0.1
- second_cols: float32 [53248], P('tensor'), may hold values from 0.01 to 0.1
Outputs:
- new_params: bfloat16 [16, 53248], P(None, 'tensor')
- next_moment: bfloat16 [16, 53248], P('fsdp', 'tensor')
- next_moment_scale: float32 [16, 416], P('fsdp', 'tensor')
- next_second: bfloat16 [16, 53248], P('fsdp', 'tensor')
- next_second_rows: float32 [16], P('fsdp')
- next_second_cols: float32 [53248], P('tensor')
Inputs may be any that keep to these rules, and one draw needn't show every extreme that they name: `grads`: partial gradients; magnitudes are at most 64.
All inputs are finite; a program needn't handle non-finite values. Where the computation divides by a largest or mean magnitude, that divisor is 1e-20 or more.
Results may differ from a plain program's by a relative error of at most 0.0004.
Values may be sent and summed in bfloat16 or wider, within the bound.
No kernel may reach another device: no remote copies, remote signals or barrier semaphores. Data moves between devices by JAX's collectives and lax.ppermute only.
A program may use at most 64 MiB of HBM per device.

v0:
```python
import math
import jax
import jax.numpy as jnp
from jax import lax
from jax.sharding import PartitionSpec as P

BLOCK = 128
STEP = 10
beta_one = 0.9
beta_two = 0.95
learn_rate = 0.01
decay_weight = 0.1
clip_rms = 0.3


def on_device(grads, params, moment_norm, moment_scale, second_norm, second_rows, second_cols):
    local = grads[0, 0].astype(jnp.float32)
    replicas = lax.psum(local, "dp")
    summed = lax.psum_scatter(replicas, "fsdp", scatter_dimension=0, tiled=True)
    own_rows, own_cols = summed.shape
    fsdp_count = lax.axis_size("fsdp")
    tensor_count = lax.axis_size("tensor")
    limit = clip_rms * math.sqrt(own_rows * fsdp_count * own_cols * tensor_count)
    total = lax.psum(jnp.sum(summed * summed), ("fsdp", "tensor"))
    factor = jnp.minimum(jnp.float32(1.0), limit / jnp.sqrt(total + 1e-06))
    clipped = factor * summed
    blocks = own_cols // BLOCK
    first_old = (
        moment_norm.astype(jnp.float32).reshape(own_rows, blocks, BLOCK) * moment_scale[:, :, None]
    ).reshape(own_rows, own_cols)
    first = beta_one * first_old + (1.0 - beta_one) * clipped
    second_old = second_norm.astype(jnp.float32) * jnp.minimum(
        second_rows[:, None], second_cols[None, :]
    )
    second = beta_two * second_old + (1.0 - beta_two) * clipped * clipped
    plain = params.astype(jnp.float32)
    ratio = first / (1.0 - beta_one**STEP) / (jnp.sqrt(second / (1.0 - beta_two**STEP)) + 1e-08)
    updated = (plain - learn_rate * (ratio + decay_weight * plain)).astype(jnp.bfloat16)
    new_params = lax.all_gather(updated, "fsdp", axis=0, tiled=True)
    grouped = first.reshape(own_rows, blocks, BLOCK)
    next_moment_scale = jnp.max(jnp.abs(grouped), axis=2)
    next_moment = (
        (grouped / (next_moment_scale[:, :, None] + 1e-06))
        .reshape(own_rows, own_cols)
        .astype(jnp.bfloat16)
    )
    row_local = jnp.max(second, axis=1)
    col_local = jnp.max(second, axis=0)
    row_peak = lax.pmax(row_local, "tensor")
    col_peak = lax.pmax(col_local, "fsdp")
    next_second = (second / jnp.minimum(row_peak[:, None], col_peak[None, :])).astype(jnp.bfloat16)
    return (new_params, next_moment, next_moment_scale, next_second, row_peak, col_peak)


def solution(mesh):
    in_specs = (
        P("dp", "fsdp", None, "tensor"),
        P("fsdp", "tensor"),
        P("fsdp", "tensor"),
        P("fsdp", "tensor"),
        P("fsdp", "tensor"),
        P("fsdp"),
        P("tensor"),
    )
    out_specs = (
        P(None, "tensor"),
        P("fsdp", "tensor"),
        P("fsdp", "tensor"),
        P("fsdp", "tensor"),
        P("fsdp"),
        P("tensor"),
    )
    return jax.shard_map(
        on_device, mesh=mesh, in_specs=in_specs, out_specs=out_specs, check_vma=False
    )
```

profile of v0, /device:TPU:0, one launch (start us, length us, event | category | flops | bytes accessed | tf_op | source)
XLA Modules:
  0.0 167.2 jit_solution(14253228319640697311)
XLA Ops:
  7.2 0.0 copy-start
  7.2 0.0 all-reduce.6.cloned.1.call-start
  7.2 2.0 %bitcast_convert_fusion = f32[16,13312]{1,0:T(8,128)} fusion(bf16[1,1,16,13312]{3,2,1,0:T(8,128)(2,1)} %param.7), kind=kLoop, calls=%fused_computation | loop fusion | flops 212992 | bytes 1277952 | tf_op jit(solution)/shard_map/convert_element_type | solution.py:17
  9.2 0.0 all-reduce.6.cloned.1.call-update
  9.2 0.0 all-reduce.4.cloned.1.call-start
  9.3 0.0 copy-start.10
  9.3 0.6 copy-done.10
  10.0 0.6 dynamic-slice
  11.2 47.7 %all-reduce.6.cloned.1.call-done = f32[16,13312]{1,0:T(8,128)} async-done(((f32[16,13312]{1,0:T(8,128)}), f32[16,13312]{1,0:T(8,128)}) %all-reduce.6.cloned.1.call-update) | async-done | bytes 851984
  58.9 1.7 %constant_dynamic-slice_fusion = f32[4,13312]{1,0:T(4,128)} fusion(f32[16,13312]{1,0:T(8,128)} %all-reduce.6.cloned.1.call-done, u32[]{:T(128)S(6)} %multiply.4), kind=kLoop, calls=%fused_computation.22 | loop fusion | bytes 425988
  60.6 0.0 copy-start.6
  60.6 0.0 all-reduce.4.cloned.1.call-update
  60.6 22.8 %all-reduce.4.cloned.1.call-done = f32[4,13312]{1,0:T(4,128)} async-done(((f32[4,13312]{1,0:T(4,128)}), f32[4,13312]{1,0:T(4,128)}) %all-reduce.4.cloned.1.call-update) | async-done | bytes 213008 | tf_op jit(solution)/shard_map/psum | solution.py:18
  83.4 0.0 copy-start.1
  83.4 1.7 %multiply_reduce_fusion = f32[]{:T(128)} fusion(f32[4,13312]{1,0:T(4,128)} %all-reduce.4.cloned.1.call-done), kind=kLoop, calls=%fused_computation.15 | loop fusion | flops 106495 | bytes 212996 | tf_op jit(solution)/shard_map/reduce_sum | solution.py:24
  85.2 0.0 copy-done
  85.2 0.0 copy-start.3
  85.2 0.0 copy-start.4
  85.2 0.1 broadcast_bitcast_fusion.1
  85.3 33.3 %psum.15 = f32[]{:T(128)} all-reduce(f32[]{:T(128)} %multiply_reduce_fusion), channel_id=1, replica_groups=mesh['dp'=2,'fsdp'=4,'tensor'=4] {'fsdp','tensor'}, use_global_device_ids=true, to_apply=%region_3.0 | all-reduce | flops 1 | bytes 8 | tf_op jit(solution)/shard_map/psum | solution.py:24
  119.3 0.0 copy-start.8
  119.3 0.0 copy-done.6
  119.3 0.0 copy-done.1
  119.3 0.0 copy-done.3
  119.3 0.0 copy-done.4
  119.3 0.6 copy-done.8
  119.9 0.5 abs_bitcast_fusion
  120.4 0.1 bitcast_reduce_fusion
  120.5 0.0 copy-start.7
  120.6 0.1 broadcast_bitcast_fusion
  120.7 0.4 copy-done.7
  121.1 0.0 copy-start.5
  121.1 16.5 %pmax.15 = f32[13312]{0:T(1024)S(1)} all-reduce(f32[13312]{0:T(1024)S(1)} %get-tuple-element.14), channel_id=1, replica_groups=mesh['dp'=2,'fsdp'=4,'tensor'=4] {'fsdp'}, use_global_device_ids=true, to_apply=%region_8.0 | all-reduce | flops 13312 | bytes 106496 | tf_op jit(solution)/shard_map/pmax | solution.py:50
  137.6 0.0 copy-start.2
  137.6 5.8 %pmax.14 = f32[4]{0:T(128)S(1)} all-reduce(f32[4]{0:T(128)S(1)} %get-tuple-element.15), channel_id=1, replica_groups=mesh['dp'=2,'fsdp'=4,'tensor'=4] {'tensor'}, use_global_device_ids=true, to_apply=%region_6.0 | all-reduce | flops 4 | bytes 32 | tf_op jit(solution)/shard_map/pmax | solution.py:49
  143.4 0.0 copy-start.9
  143.4 0.5 copy-done.9
  143.9 0.0 copy-done.5
  143.9 1.0 fusion.6
  144.9 0.0 copy-done.2
  144.9 14.6 %all-gather = bf16[4,4,13312]{2,1,0:T(4,128)(2,1)S(1)} all-gather(bf16[1,4,13312]{2,1,0:T(4,128)(2,1)S(1)} %get-tuple-element.12), channel_id=1, replica_groups=mesh['dp'=2,'fsdp'=4,'tensor'=4] {'fsdp'}, dimensions={0}, use_global_device_ids=true | all-gather | bytes 532480 | tf_op jit(solution)/shard_map/all_gather | solution.py:39
  159.5 0.9 reshape.32
  (1 shorter events, 0.0 us)
Async XLA Ops:
  7.2 78.0 %copy-start = (f32[4,104]{1,0:T(4,128)S(1)}, f32[4,104]{1,0:T(4,128)}, u32[]{:S(2)}) copy-start(f32[4,104]{1,0:T(4,128)} %param.10) | copy-start | bytes 4996
  7.2 51.7 %all-reduce.6.cloned.1.call-start = ((), (), s32[]{:S(2)}) async-start(), calls=%async_computation.1 | async-start | bytes 1703936
  9.2 74.2 %all-reduce.4.cloned.1.call-start = ((), (), s32[]{:S(2)}) async-start(), calls=%async_computation | async-start | bytes 425984 | tf_op jit(solution)/shard_map/psum | solution.py:18
  9.3 0.7 copy-start.10
  60.6 58.7 %copy-start.6 = (f32[13312]{0:T(1024)S(1)}, f32[13312]{0:T(1024)}, u32[]{:S(2)}) copy-start(f32[13312]{0:T(1024)} %param.13) | copy-start | bytes 159748
  83.4 35.9 %copy-start.1 = (f32[4,13312]{1,0:T(4,128)S(1)}, f32[4,13312]{1,0:T(4,128)}, u32[]{:S(2)}) copy-start(f32[4,13312]{1,0:T(4,128)} %all-reduce.4.cloned.1.call-done) | copy-start | bytes 638980
  85.2 34.1 %copy-start.3 = (bf16[4,13312]{1,0:T(4,128)(2,1)S(1)}, bf16[4,13312]{1,0:T(4,128)(2,1)}, u32[]{:S(2)}) copy-start(bf16[4,13312]{1,0:T(4,128)(2,1)} %param.9) | copy-start | bytes 319492
  85.2 34.1 %copy-start.4 = (bf16[4,13312]{1,0:T(4,128)(2,1)S(1)}, bf16[4,13312]{1,0:T(4,128)(2,1)}, u32[]{:S(2)}) copy-start(bf16[4,13312]{1,0:T(4,128)(2,1)} %param.11) | copy-start | bytes 319492
  119.3 0.7 copy-start.8
  120.5 0.6 copy-start.7
  121.1 22.8 %copy-start.5 = (bf16[4,13312]{1,0:T(4,128)(2,1)S(1)}, bf16[4,13312]{1,0:T(4,128)(2,1)}, u32[]{:S(2)}) copy-start(bf16[4,13312]{1,0:T(4,128)(2,1)} %param.8) | copy-start | bytes 319492
  137.6 7.3 %copy-start.2 = (f32[13312]{0:T(1024)}, f32[13312]{0:T(1024)S(1)}, u32[]{:S(2)}) copy-start(f32[13312]{0:T(1024)S(1)} %pmax.15) | copy-start | bytes 159748
  143.4 0.5 copy-start.9
Sparse Core Ops, SparseCore 0:
  10.4 48.4 all-reduce.5
  61.7 21.6 all-reduce.3
where the time goes:
time: 168 us; the launch traced here: 167 us
  waiting for transfers between devices  70.5 us (42%)
  blocking collectives  70.1 us (42%)
  between operations  15.5 us (9%)
  local copies, waits for them, and re-layouts  5.64 us (3%)
  other arithmetic  5.35 us (3%)
    unnamed x3, waiting for transfers between devices  47.7 us
    psum x1, blocking collectives, on_device(): total = lax.psum(jnp.sum(summed * summed), ('fsdp', 'tensor'))  33.3 us
    psum x1, waiting for transfers between devices, on_device(): replicas = lax.psum(local, 'dp')  22.8 us
    pmax x1, blocking collectives, on_device(): col_peak = lax.pmax(col_local, 'fsdp')  16.5 us
    all_gather x1, blocking collectives, on_device(): new_params = lax.all_gather(updated, 'fsdp', axis=0, tiled=True)  14.6 us
    pmax x1, blocking collectives, on_device(): row_peak = lax.pmax(row_local, 'tensor')  5.76 us
    unnamed x27, local copies, waits for them, and re-layouts  5.64 us
  transfers between devices with their start and end apart: 2, of which 2 were waited for; matrix products, arithmetic and copies ran while one was open for 0% of the time, Pallas kernels for 0%

commit v1 on v0

--- a/solution.py
+++ b/solution.py
@@ -15,7 +15,7 @@
 
 def on_device(grads, params, moment_norm, moment_scale, second_norm, second_rows, second_cols):
     local = grads[0, 0].astype(jnp.float32)
-    replicas = lax.psum(local, "dp")
+    replicas = local + lax.ppermute(local, "dp", [(0, 1), (1, 0)])
     summed = lax.psum_scatter(replicas, "fsdp", scatter_dimension=0, tiled=True)
     own_rows, own_cols = summed.shape
     fsdp_count = lax.axis_size("fsdp")

time: 168 us -> 162 us (0.964)
  waiting for transfers between devices: 70.5 us -> 64.5 us
  starting transfers between devices: 0.08 us -> 3.07 us
  local copies, waits for them, and re-layouts: 5.64 us -> 3.93 us
  blocking collectives: 70.1 us -> 68.4 us
    psum x1 -> x0, waiting for transfers between devices: 22.8 us -> none  [on_device(): replicas = lax.psum(local, 'dp')]
    ppermute x0 -> x1, waiting for transfers between devices: none -> 18.9 us  [on_device(): replicas = local + lax.ppermute(local, 'dp', [(0, 1), (1, 0)])]
    ppermute x0 -> x1, starting transfers between devices: none -> 3.03 us  [on_device(): replicas = local + lax.ppermute(local, 'dp', [(0, 1), (1, 0)])]
    unnamed x3 -> x2, waiting for transfers between devices: 47.7 us -> 45.5 us
    unnamed x27 -> x26, local copies, waits for them, and re-layouts: 5.64 us -> 3.93 us
where the time goes in v1:
time: 162 us
  blocking collectives  68.4 us (42%)
  waiting for transfers between devices  64.5 us (40%)
  between operations  15.5 us (10%)
  other arithmetic  6.52 us (4%)
  local copies, waits for them, and re-layouts  3.93 us (2%)
  starting transfers between devices  3.07 us (2%)
    unnamed x2, waiting for transfers between devices  45.5 us
    psum x1, blocking collectives, on_device(): total = lax.psum(jnp.sum(summed * summed), ('fsdp', 'tensor'))  31.7 us
    ppermute x1, waiting for transfers between devices, on_device(): replicas = local + lax.ppermute(local, 'dp', [(0, 1), (1, 0)])  18.9 us
    pmax x1, blocking collectives, on_device(): col_peak = lax.pmax(col_local, 'fsdp')  16.5 us
    all_gather x1, blocking collectives, on_device(): new_params = lax.all_gather(updated, 'fsdp', axis=0, tiled=True)  14.6 us
    pmax x1, blocking collectives, on_device(): row_peak = lax.pmax(row_local, 'tensor')  5.76 us
    unnamed x26, local copies, waits for them, and re-layouts  3.93 us
  transfers between devices with their start and end apart: 2, of which 2 were waited for; matrix products, arithmetic and copies ran while one was open for 0% of the time, Pallas kernels for 0%

profile of v1, /device:TPU:0, one launch (start us, length us, event | category | flops | bytes accessed | tf_op | source)
XLA Modules:
  0.0 161.9 jit_solution(13113985034681718000)
XLA Ops:
  7.2 0.0 copy-start
  7.2 0.0 copy-start.1
  7.2 0.0 all-reduce.3.cloned.1.call-start
  7.2 1.1 bitcast_convert_fusion
  8.3 3.0 %collective-permute-start = (f32[16,13312]{1,0:T(8,128)S(1)}, f32[16,13312]{1,0:T(8,128)S(1)}, u32[]{:S(2)}, u32[]{:S(2)}) collective-permute-start(f32[16,13312]{1,0:T(8,128)S(1)} %bitcast_convert_fusion), channel_id=1, source_target_pairs={{0,16},{16,0},{1,17},{17,1},{2,18},{18,2},{3,19},{19,3},{4,20},{20... | collective-permute-start | bytes 2555912 | tf_op jit(solution)/shard_map/ppermute | solution.py:18
  11.4 18.9 %collective-permute-done = f32[16,13312]{1,0:T(8,128)S(1)} collective-permute-done((f32[16,13312]{1,0:T(8,128)S(1)}, f32[16,13312]{1,0:T(8,128)S(1)}, u32[]{:S(2)}, u32[]{:S(2)}) %collective-permute-start) | collective-permute-done | bytes 852000 | tf_op jit(solution)/shard_map/ppermute | solution.py:18
  30.3 0.0 copy-done.1
  30.3 1.0 fusion.4
  31.3 0.0 all-reduce.3.cloned.1.call-update
  31.4 0.0 copy-start.10
  31.4 0.6 copy-done.10
  32.0 0.6 dynamic-slice
  33.2 45.5 %all-reduce.3.cloned.1.call-done = f32[16,13312]{1,0:T(8,128)} async-done(((f32[16,13312]{1,0:T(8,128)}), f32[16,13312]{1,0:T(8,128)}) %all-reduce.3.cloned.1.call-update) | async-done | bytes 851984
  78.8 0.0 copy-start.6
  78.8 1.7 %multiply_reduce_fusion = f32[]{:T(128)} fusion(f32[16,13312]{1,0:T(8,128)} %all-reduce.3.cloned.1.call-done, u32[]{:T(128)S(6)} %multiply.4), kind=kLoop, calls=%fused_computation.16 | loop fusion | flops 106495 | bytes 213000 | tf_op jit(solution)/shard_map/reduce_sum | solution.py:24
  80.5 0.0 copy-done
  80.5 0.0 copy-start.3
  80.5 0.0 copy-start.4
  80.5 0.1 broadcast_bitcast_fusion.1
  80.6 31.7 %psum.7 = f32[]{:T(128)} all-reduce(f32[]{:T(128)} %multiply_reduce_fusion), channel_id=1, replica_groups=mesh['dp'=2,'fsdp'=4,'tensor'=4] {'fsdp','tensor'}, use_global_device_ids=true, to_apply=%region_2.0 | all-reduce | flops 1 | bytes 8 | tf_op jit(solution)/shard_map/psum | solution.py:24
  113.0 0.0 copy-start.8
  113.0 0.0 copy-done.6
  113.0 0.0 copy-done.3
  113.0 0.0 copy-done.4
  113.0 0.6 copy-done.8
  113.6 1.5 abs_bitcast_fusion
  115.1 0.1 bitcast_reduce_fusion
  115.3 0.0 copy-start.7
  115.3 0.1 broadcast_bitcast_fusion
  115.4 0.4 copy-done.7
  115.9 0.0 copy-start.5
  115.9 16.5 %pmax.15 = f32[13312]{0:T(1024)S(1)} all-reduce(f32[13312]{0:T(1024)S(1)} %get-tuple-element.11), channel_id=1, replica_groups=mesh['dp'=2,'fsdp'=4,'tensor'=4] {'fsdp'}, use_global_device_ids=true, to_apply=%region_7.0 | all-reduce | flops 13312 | bytes 106496 | tf_op jit(solution)/shard_map/pmax | solution.py:50
  132.3 0.0 copy-start.2
  132.3 5.8 %pmax.14 = f32[4]{0:T(128)S(1)} all-reduce(f32[4]{0:T(128)S(1)} %get-tuple-element.12), channel_id=1, replica_groups=mesh['dp'=2,'fsdp'=4,'tensor'=4] {'tensor'}, use_global_device_ids=true, to_apply=%region_5.0 | all-reduce | flops 4 | bytes 32 | tf_op jit(solution)/shard_map/pmax | solution.py:49
  138.1 0.0 copy-start.9
  138.1 0.5 copy-done.9
  138.6 0.0 copy-done.5
  138.6 1.0 fusion.7
  139.6 0.0 copy-done.2
  139.7 14.6 %all-gather = bf16[4,4,13312]{2,1,0:T(4,128)(2,1)S(1)} all-gather(bf16[1,4,13312]{2,1,0:T(4,128)(2,1)S(1)} %get-tuple-element.15), channel_id=1, replica_groups=mesh['dp'=2,'fsdp'=4,'tensor'=4] {'fsdp'}, dimensions={0}, use_global_device_ids=true | all-gather | bytes 532480 | tf_op jit(solution)/shard_map/all_gather | solution.py:39
  154.2 0.9 reshape.32
  (1 shorter events, 0.0 us)
Async XLA Ops:
  7.2 73.3 %copy-start = (f32[4,104]{1,0:T(4,128)S(1)}, f32[4,104]{1,0:T(4,128)}, u32[]{:S(2)}) copy-start(f32[4,104]{1,0:T(4,128)} %param.10) | copy-start | bytes 4996
  7.2 23.1 %copy-start.1 = (bf16[1,1,16,13312]{3,2,1,0:T(8,128)(2,1)S(1)}, bf16[1,1,16,13312]{3,2,1,0:T(8,128)(2,1)}, u32[]{:S(2)}) copy-start(bf16[1,1,16,13312]{3,2,1,0:T(8,128)(2,1)} %param.7) | copy-start | bytes 1277956
  7.2 71.6 %all-reduce.3.cloned.1.call-start = ((), (), s32[]{:S(2)}) async-start(), calls=%async_computation | async-start | bytes 1703936
  8.3 22.0 %collective-permute-start = (f32[16,13312]{1,0:T(8,128)S(1)}, f32[16,13312]{1,0:T(8,128)S(1)}, u32[]{:S(2)}, u32[]{:S(2)}) collective-permute-start(f32[16,13312]{1,0:T(8,128)S(1)} %bitcast_convert_fusion), channel_id=1, source_target_pairs={{0,16},{16,0},{1,17},{17,1},{2,18},{18,2},{3,19},{19,3},{4,20},{20... | collective-permute-start | bytes 2555912 | tf_op jit(solution)/shard_map/ppermute | solution.py:18
  31.4 0.7 copy-start.10
  78.8 34.2 %copy-start.6 = (f32[13312]{0:T(1024)S(1)}, f32[13312]{0:T(1024)}, u32[]{:S(2)}) copy-start(f32[13312]{0:T(1024)} %param.13) | copy-start | bytes 159748
  80.5 32.5 %copy-start.3 = (bf16[4,13312]{1,0:T(4,128)(2,1)S(1)}, bf16[4,13312]{1,0:T(4,128)(2,1)}, u32[]{:S(2)}) copy-start(bf16[4,13312]{1,0:T(4,128)(2,1)} %param.9) | copy-start | bytes 319492
  80.5 32.5 %copy-start.4 = (bf16[4,13312]{1,0:T(4,128)(2,1)S(1)}, bf16[4,13312]{1,0:T(4,128)(2,1)}, u32[]{:S(2)}) copy-start(bf16[4,13312]{1,0:T(4,128)(2,1)} %param.11) | copy-start | bytes 319492
  113.0 0.7 copy-start.8
  115.3 0.6 copy-start.7
  115.9 22.8 %copy-start.5 = (bf16[4,13312]{1,0:T(4,128)(2,1)S(1)}, bf16[4,13312]{1,0:T(4,128)(2,1)}, u32[]{:S(2)}) copy-start(bf16[4,13312]{1,0:T(4,128)(2,1)} %param.8) | copy-start | bytes 319492
  132.3 7.3 %copy-start.2 = (f32[13312]{0:T(1024)}, f32[13312]{0:T(1024)S(1)}, u32[]{:S(2)}) copy-start(f32[13312]{0:T(1024)S(1)} %pmax.15) | copy-start | bytes 159748
  138.1 0.5 copy-start.9
Sparse Core Ops, SparseCore 0:
  31.5 47.2 all-reduce.2
